TPU v7x, 32 devices: a whole 2x2x4 slice. The times are simulated.
32 devices in a mesh: comp: 2 (over core), dom: 16 (over z, y, x).
Axes of the slice: x: 2, y: 2, z: 4, core: 2. Of those that a mesh axis runs over, the one named last changes fastest.
Arguments:
- surface_flux: float32 [6, 12, 131072], P(None, None, ('comp', 'dom')), may hold values from -8 to 8
- active_mask: int32 [131072], P(('comp', 'dom')), may hold values 0 or 1
- source_area: float32 [131072], P(('comp', 'dom')), may hold values from 0.5 to 30
- tile_targets: int32 [2048, 2], P(('comp', 'dom')), may hold values from 0 to 31, all different within a row
- remap_tiles: float32 [2048, 2, 64, 384], P(('comp', 'dom')), may hold values from -0.0625 to 0.0625
- ocean_flux: float32 [12, 12288], P(None, ('comp', 'dom')), may hold values from -6 to 6
- air_fraction: float32 [3, 12288], P(None, ('comp', 'dom')), may hold values from 0 to 1, as said below
- air_area: float32 [12288], P(('comp', 'dom')), may hold values from 0.5 to 30
Outputs:
- merged: float32 [12, 12288], P(None, ('comp', 'dom'))
- area_means: float32 [3, 12], replicated
Inputs may be any that keep to these rules, and one draw needn't show every extreme that they name: `air_fraction`: the three fractions of a cell are positive and sum to one. `tile_targets`: the 2 targets of one source block differ.
All inputs are finite; a program needn't handle non-finite values. No bound on the sum of `active_mask` on one device may be relied on, other than what follows from the above.
Results may differ from a plain program's by a relative error of at most 0.000071.
Values sent between devices are 32-bit elements; how exact they have to be, the bound alone decides.
No kernel may reach another device: no remote copies, remote signals or barrier semaphores. Data moves between devices by JAX's collectives and lax.ppermute only.
A program may use at most 64 MiB of HBM per device.

v0:
```python
import jax
import jax.numpy as jnp
from jax import lax
from jax.sharding import PartitionSpec as P


def on_device(
    surface_flux,
    active_mask,
    source_area,
    tile_targets,
    remap_tiles,
    ocean_flux,
    air_fraction,
    air_area,
):
    step_count = surface_flux.shape[0]
    field_count = surface_flux.shape[1]
    block_count, intersection, block_cells, air_cells = remap_tiles.shape
    group_count = lax.axis_size("comp")
    domain_count = lax.axis_size("dom")
    owner_count = group_count * domain_count
    coverage = active_mask.astype(jnp.float32) * source_area
    average = jnp.sum(surface_flux, axis=0) / step_count
    weighted = average * coverage[None, :]
    blocks = weighted.reshape(field_count, block_count, block_cells)
    contrib = jnp.einsum("fbs,btsa->btfa", blocks, remap_tiles, precision=lax.Precision.HIGHEST)
    contrib = contrib.reshape(block_count * intersection, field_count * air_cells)
    targets = tile_targets.reshape(block_count * intersection)
    own_group = lax.axis_index("comp")
    group_pick = (jnp.arange(group_count, dtype=jnp.int32) == own_group).astype(jnp.float32)
    surface_num = group_pick[:, None] * jnp.sum(weighted, axis=1)[None, :]
    surface_den = group_pick * jnp.sum(source_area)
    owner_ids = jnp.arange(owner_count, dtype=jnp.int32)
    selector = (targets[None, :] == owner_ids[:, None]).astype(jnp.float32)
    outgoing = jnp.dot(selector, contrib, precision=lax.Precision.HIGHEST)
    incoming = lax.all_to_all(outgoing, ("comp", "dom"), split_axis=0, concat_axis=0, tiled=True)
    owner_sums = jnp.sum(
        incoming.reshape(group_count, domain_count, field_count * air_cells), axis=1
    )
    remapped = owner_sums.reshape(group_count, field_count, air_cells) / air_area[None, None, :]
    merged = (
        air_fraction[0][None, :] * remapped[0]
        + air_fraction[1][None, :] * remapped[1]
        + air_fraction[2][None, :] * ocean_flux
    )
    air_num = jnp.sum(merged * air_area[None, :], axis=1)
    air_den = jnp.sum(air_area)
    joined = lax.psum(
        (
            jnp.concatenate([surface_num, air_num[None, :]], axis=0),
            jnp.concatenate([surface_den, air_den[None]], axis=0),
        ),
        ("comp", "dom"),
    )
    numerators = joined[0]
    denominators = joined[1]
    area_means = numerators / denominators[:, None]
    return (merged, area_means)


def solution(mesh):
    in_specs = (
        P(None, None, ("comp", "dom")),
        P(("comp", "dom")),
        P(("comp", "dom")),
        P(("comp", "dom"), None),
        P(("comp", "dom"), None, None, None),
        P(None, ("comp", "dom")),
        P(None, ("comp", "dom")),
        P(("comp", "dom")),
    )
    out_specs = (P(None, ("comp", "dom")), P())
    return jax.shard_map(
        on_device, mesh=mesh, in_specs=in_specs, out_specs=out_specs, check_vma=False
    )
```

profile of v0, /device:TPU:0, one launch (start us, length us, event | category | flops | bytes accessed | tf_op | source)
XLA Modules:
  0.0 81.3 jit_solution(15840653103286598785)
XLA Ops:
  0.6 1.3 %fusion.8 = (f32[]{:T(128)}, f32[4096]{0:T(1024)S(1)}) fusion(f32[4096]{0:T(1024)} %param.10, s32[4096]{0:T(1024)} %param.9), kind=kLoop, calls=%fused_computation.25 | loop fusion | flops 16383 | bytes 49156 | tf_op jit(solution)/shard_map/reduce_sum | solution.py:33
  2.0 0.1 mul.84
  2.0 0.8 copy.13
  2.8 0.1 eq.25
  3.0 1.5 %reduce_sum.56 = f32[12,4096]{1,0:T(8,128)S(1)} reduce(f32[6,12,4096]{2,1,0:T(8,128)} %param.8, f32[]{:T(128)} %constant.8.clone.1), dimensions={0}, to_apply=%region_0.0 | reduce | flops 245760 | bytes 1376260 | tf_op jit(solution)/shard_map/reduce_sum | solution.py:24
  4.5 0.2 reduce_sum.57
  4.7 9.2 %fusion = f32[64,12,2,384]{3,1,2,0:T(8,128)S(1)} fusion(f32[64,2,64,384]{3,2,1,0:T(8,128)} %param.12, f32[12,64,64,1]{2,1,0,3:T(8,128)S(1)} %multiply_bitcast_fusion), kind=kOutput, calls=%fused_computation.1 | convolution fusion | flops 452984832 | bytes 15138816 | tf_op jit(solution)/shard_map/fbs,btsa->btfa/dot_general | solution.py:27
  13.8 0.7 copy.20
  14.6 0.0 copy-start.1
  14.6 0.0 copy-start.2
  14.6 0.0 copy-start
  14.6 1.0 %convolution_bitcast_fusion = f32[32,1,4608]{2,0,1:T(8,128)S(1)} fusion(f32[128,4608]{1,0:T(8,128)S(1)} %bitcast.30, s32[128]{0:T(128)S(1)} %eq.25), kind=kOutput, calls=%fused_computation | convolution fusion | flops 226496512 | bytes 2949632 | tf_op jit(solution)/shard_map/dot_general | solution.py:36
  15.6 1.4 %copy.15 = f32[32,1,4608]{2,1,0:T(1,128)} copy(f32[32,1,4608]{2,0,1:T(8,128)S(1)} %convolution_bitcast_fusion) | data formatting | bytes 1179648 | tf_op jit(solution)/shard_map/all_to_all | solution.py:37
  17.0 7.3 %all-to-all-start = ((f32[32,1,4608]{2,1,0:T(1,128)}), f32[32,1,4608]{2,1,0:T(1,128)S(1)}, u32[]{:S(2)}, u32[]{:S(2)}) async-start(f32[32,1,4608]{2,1,0:T(1,128)} %copy.15), calls=%async_computation | async-start | bytes 1179648 | tf_op jit(solution)/shard_map/all_to_all | solution.py:37
  24.4 0.0 copy-done.1
  24.4 0.6 reduce_sum.62
  25.0 0.6 compare_select_fusion
  25.6 0.7 pad_maximum_fusion.1
  26.3 0.0 copy-done.2
  26.4 0.1 multiply_reduce_fusion
  26.5 0.1 broadcast_multiply_fusion
  26.6 16.0 %all-to-all-done = f32[32,1,4608]{2,1,0:T(1,128)S(1)} async-done(((f32[32,1,4608]{2,1,0:T(1,128)}), f32[32,1,4608]{2,1,0:T(1,128)S(1)}, u32[]{:S(2)}, u32[]{:S(2)}) %all-to-all-start) | async-done | bytes 589856 | tf_op jit(solution)/shard_map/all_to_all | solution.py:37
  42.6 0.1 reduce_sum.58
  42.8 0.0 copy-done
  42.8 0.7 multiply_reduce_fusion.1
  43.5 37.1 %all-reduce = (f32[3,12]{1,0:T(4,128)S(1)}, f32[3]{0:T(128)S(1)}) all-reduce(f32[3,12]{1,0:T(4,128)S(1)} %pad_maximum_fusion, f32[3]{0:T(128)S(1)} %pad_maximum_fusion.1), channel_id=1, replica_groups=mesh['comp'=2,'dom'=16] {'comp','dom'}, use_global_device_ids=true, to_apply=%region_4.0 | all-reduce | flops 39 | bytes 312 | tf_op jit(solution)/shard_map/psum | solution.py:49
  80.7 0.7 broadcast_divide_fusion.1
  (7 shorter events, 0.2 us)
Async XLA Ops:
  14.6 9.8 %copy-start.1 = (f32[384]{0:T(512)S(1)}, f32[384]{0:T(512)}, u32[]{:S(2)}) copy-start(f32[384]{0:T(512)} %param.15) | copy-start | bytes 4612
  14.6 11.7 %copy-start.2 = (f32[3,384]{1,0:T(4,128)S(1)}, f32[3,384]{1,0:T(4,128)}, u32[]{:S(2)}) copy-start(f32[3,384]{1,0:T(4,128)} %param.14) | copy-start | bytes 13828
  14.6 28.1 %copy-start = (f32[12,384]{1,0:T(8,128)S(1)}, f32[12,384]{1,0:T(8,128)}, u32[]{:S(2)}) copy-start(f32[12,384]{1,0:T(8,128)} %param.13) | copy-start | bytes 55300
  17.0 25.5 %all-to-all-start = ((f32[32,1,4608]{2,1,0:T(1,128)}), f32[32,1,4608]{2,1,0:T(1,128)S(1)}, u32[]{:S(2)}, u32[]{:S(2)}) async-start(f32[32,1,4608]{2,1,0:T(1,128)} %copy.15), calls=%async_computation | async-start | bytes 1179648 | tf_op jit(solution)/shard_map/all_to_all | solution.py:37
where the time goes:
time: 82.1 us; the launch traced here: 81.3 us
  blocking collectives  37.1 us (45%)
  waiting for transfers between devices  16 us (19%)
  matrix products  10.1 us (12%)
  starting transfers between devices  7.33 us (9%)
  other arithmetic  6.6 us (8%)
  local copies, waits for them, and re-layouts  3.41 us (4%)
    psum x1, blocking collectives, on_device(): lax.psum((jnp.concatenate([surface_num, air_num[None, :]], axis=0), jnp.c...  37.1 us
    all_to_all x1, waiting for transfers between devices, on_device(): lax.all_to_all(outgoing, ('comp', 'dom'), split_axis=0, concat_axis=0, ti...  16 us
    dot_general x1, matrix products, on_device(): jnp.einsum('fbs,btsa->btfa', blocks, remap_tiles, precision=lax.Precision...  9.16 us
    all_to_all x1, starting transfers between devices, on_device(): lax.all_to_all(outgoing, ('comp', 'dom'), split_axis=0, concat_axis=0, ti...  7.33 us
  transfers between devices with their start and end apart: 1, of which 1 were waited for; matrix products, arithmetic and copies ran while one was open for 3% of the time, Pallas kernels for 0%

commit v1 on v0

v1 whole, which is shorter than its diff:
```python
import functools

import jax
import jax.numpy as jnp
from jax import lax
from jax.experimental import pallas as pl
from jax.experimental.pallas import tpu as pltpu
from jax.sharding import PartitionSpec as P

QUAD = 4
STEP_BLOCKS = 8
ROWS = 16


def split(x):
    hi = x.astype(jnp.bfloat16)
    lo = (x - hi.astype(jnp.float32)).astype(jnp.bfloat16)
    return hi, lo


def own_position():
    return lax.axis_index("comp") * lax.axis_size("dom") + lax.axis_index("dom")


def phase_plan(domain_count):
    plan, stride = [], 1
    while stride < domain_count:
        radix = 4 if domain_count // stride >= 4 else 2
        plan.append((radix, stride))
        stride *= radix
    return plan


def chunk_order(domain_count):
    order = [0]
    for radix, stride in reversed(phase_plan(domain_count)):
        order = [digit * stride + rest for digit in range(radix) for rest in order]
    return order


def remap_kernel(targets, flux, mask, area, tiles, sums, weighted_sum, padded):
    step = pl.program_id(0)
    me = own_position()
    step_count, field_count, _ = flux.shape
    block_cells = tiles.shape[2]
    air_cells = tiles.shape[3]
    cells = QUAD * block_cells
    lanes = mask.shape[1]

    @pl.when(step == 0)
    def _():
        sums[...] = jnp.zeros_like(sums)
        weighted_sum[...] = jnp.zeros_like(weighted_sum)
        padded[...] = jnp.zeros_like(padded)

    row_block = lax.broadcasted_iota(jnp.int32, (QUAD * ROWS, cells), 0) // ROWS
    col_block = lax.broadcasted_iota(jnp.int32, (QUAD * ROWS, cells), 1) // block_cells
    diagonal = row_block == col_block
    for quad in range(STEP_BLOCKS // QUAD):
        for part in range(cells // lanes):
            start = quad * cells + part * lanes
            row = step * (STEP_BLOCKS * block_cells // lanes) + start // lanes
            total = flux[0, :, start : start + lanes]
            for s in range(1, step_count):
                total = total + flux[s, :, start : start + lanes]
            coverage = mask[pl.ds(row, 1), :].astype(jnp.float32) * area[pl.ds(row, 1), :]
            weighted = (total / step_count) * coverage
            weighted_sum[0:field_count, :] += weighted
            padded[quad, 0:field_count, part * lanes : (part + 1) * lanes] = weighted
        value = padded[quad]
        left = jnp.where(diagonal, jnp.concatenate([value] * QUAD, axis=0), 0.0)
        left_hi, left_lo = split(left)
        left_both = jnp.concatenate([left_hi, left_lo], axis=0)
        for slot in range(tiles.shape[1]):
            right = tiles[quad * QUAD : (quad + 1) * QUAD, slot].reshape(cells, air_cells)
            right_hi, right_lo = split(right)
            first = jnp.dot(left_both, right_hi, preferred_element_type=jnp.float32)
            second = jnp.dot(left_hi, right_lo, preferred_element_type=jnp.float32)
            made = first[: QUAD * ROWS] + (first[QUAD * ROWS :] + second)
            for b in range(QUAD):
                target = targets[slot, step * STEP_BLOCKS + quad * QUAD + b]
                sums[target ^ me] += made[b * ROWS : (b + 1) * ROWS]


def as_row(column, width):
    eye = lax.broadcasted_iota(jnp.int32, (column.shape[0], width), 0) == lax.broadcasted_iota(
        jnp.int32, (column.shape[0], width), 1
    )
    return jnp.sum(jnp.where(eye, column, 0.0), axis=0, keepdims=True)


def weigh_kernel(order, sums, weighted_sum, shares, area, ocean, fraction, air_area, keep, send):
    me = own_position()
    own_group = lax.axis_index("comp")
    domain_count = len(order)
    field_count, width = ocean.shape
    total = jnp.zeros(sums.shape[1:], jnp.float32)
    for owner in range(2 * domain_count):
        total = total + sums[owner] * shares[owner ^ me]
    ocean_term = fraction[2:3, :] * ocean[...] * air_area[...]
    air_num = as_row(jnp.sum(total, axis=1, keepdims=True), width) + as_row(
        jnp.sum(ocean_term, axis=1, keepdims=True), width
    )
    air_den = jnp.sum(air_area[...])
    surface_num = as_row(jnp.sum(weighted_sum[...], axis=1, keepdims=True), width)
    surface_den = jnp.sum(area[...])
    lane = lax.broadcasted_iota(jnp.int32, (1, width), 1)
    surface = jnp.where(lane == field_count, surface_den, surface_num)
    air = jnp.where(lane == field_count, air_den, air_num)
    row = lax.broadcasted_iota(jnp.int32, (ROWS, width), 0)
    extra = jnp.where(row == field_count + own_group, surface, 0.0)
    extra = jnp.where(row == field_count + 2, air, extra)
    for slot, place in enumerate(order):
        keep[slot] = sums[place] * shares[place ^ me] + extra
        far = domain_count + place
        send[slot] = sums[far] * shares[far ^ me] + extra


def merge_kernel(*refs):
    pieces, (ocean, fraction, air_area, merged, means) = refs[:-5], refs[-5:]
    field_count = ocean.shape[0]
    total = tree_sum([piece[0] for piece in pieces])
    merged[...] = total[:field_count] / air_area[...] + fraction[2:3, :] * ocean[...]
    rows = total[field_count : field_count + 3]
    means[...] = rows[:, :field_count] / rows[:, field_count : field_count + 1]


def tree_sum(items):
    while len(items) > 1:
        items = [items[i] + items[i + 1] for i in range(0, len(items), 2)]
    return items[0]


def exchange(chunks, radix, stride):
    domain_count = lax.axis_size("dom")
    part = chunks.shape[0] // radix
    pieces = [chunks[:part]]
    for digit in range(1, radix):
        pairs = [(i, i ^ (digit * stride)) for i in range(domain_count)]
        pieces.append(lax.ppermute(chunks[digit * part : (digit + 1) * part], "dom", pairs))
    return pieces


def on_device(
    surface_flux,
    active_mask,
    source_area,
    tile_targets,
    remap_tiles,
    ocean_flux,
    air_fraction,
    air_area,
):
    step_count, field_count, cell_count = surface_flux.shape
    block_count, intersection, block_cells, air_cells = remap_tiles.shape
    group_count = lax.axis_size("comp")
    domain_count = lax.axis_size("dom")
    owner_count = group_count * domain_count
    lanes = 128
    order = chunk_order(domain_count)
    vmem = pl.BlockSpec(memory_space=pltpu.VMEM)

    mask = active_mask.reshape(cell_count // lanes, lanes)
    area = source_area.reshape(cell_count // lanes, lanes)
    air_row = air_area.reshape(1, air_cells)

    spread = jnp.broadcast_to(
        air_fraction[:group_count, None, None, :], (group_count, domain_count, 1, air_cells)
    ).reshape(owner_count, 1, air_cells)
    shares = lax.all_to_all(spread, ("comp", "dom"), split_axis=0, concat_axis=0, tiled=True)

    step_cells = STEP_BLOCKS * block_cells
    sums, weighted_sum = pl.pallas_call(
        remap_kernel,
        grid=(block_count // STEP_BLOCKS,),
        in_specs=[
            pl.BlockSpec(memory_space=pltpu.SMEM),
            pl.BlockSpec((step_count, field_count, step_cells), lambda i: (0, 0, i)),
            pl.BlockSpec((cell_count // lanes, lanes), lambda i: (0, 0)),
            pl.BlockSpec((cell_count // lanes, lanes), lambda i: (0, 0)),
            pl.BlockSpec((STEP_BLOCKS, intersection, block_cells, air_cells), lambda i: (i, 0, 0, 0)),
        ],
        out_specs=[
            pl.BlockSpec((owner_count, ROWS, air_cells), lambda i: (0, 0, 0)),
            pl.BlockSpec((ROWS, lanes), lambda i: (0, 0)),
        ],
        out_shape=[
            jax.ShapeDtypeStruct((owner_count, ROWS, air_cells), jnp.float32),
            jax.ShapeDtypeStruct((ROWS, lanes), jnp.float32),
        ],
        scratch_shapes=[
            pltpu.VMEM((STEP_BLOCKS // QUAD, ROWS, QUAD * block_cells), jnp.float32)
        ],
        cost_estimate=pl.CostEstimate(
            flops=2 * 16 * 6 * remap_tiles.size, bytes_accessed=4 * remap_tiles.size, transcendentals=0
        ),
        name="remap",
    )(tile_targets.T, surface_flux, mask, area, remap_tiles)

    half = jax.ShapeDtypeStruct((domain_count, ROWS, air_cells), jnp.float32)
    keep, send = pl.pallas_call(
        functools.partial(weigh_kernel, order),
        in_specs=[vmem] * 7,
        out_specs=[vmem] * 2,
        out_shape=[half, half],
        name="weigh",
    )(sums, weighted_sum, shares, area, ocean_flux, air_fraction, air_row)

    pairs = [(i, i ^ 1) for i in range(group_count)]
    chunks = keep + lax.ppermute(send, "comp", pairs)
    pieces = [chunks]
    for radix, stride in phase_plan(domain_count):
        pieces = exchange(tree_sum(pieces), radix, stride)

    merged, means = pl.pallas_call(
        merge_kernel,
        in_specs=[vmem] * (len(pieces) + 3),
        out_specs=[vmem] * 2,
        out_shape=[
            jax.ShapeDtypeStruct((field_count, air_cells), jnp.float32),
            jax.ShapeDtypeStruct((group_count + 1, field_count), jnp.float32),
        ],
        name="merge",
    )(*pieces, ocean_flux, air_fraction, air_row)
    return (merged, means)


def solution(mesh):
    in_specs = (
        P(None, None, ("comp", "dom")),
        P(("comp", "dom")),
        P(("comp", "dom")),
        P(("comp", "dom"), None),
        P(("comp", "dom"), None, None, None),
        P(None, ("comp", "dom")),
        P(None, ("comp", "dom")),
        P(("comp", "dom")),
    )
    out_specs = (P(None, ("comp", "dom")), P())
    return jax.shard_map(
        on_device, mesh=mesh, in_specs=in_specs, out_specs=out_specs, check_vma=False
    )
```

time: 82.1 us -> 45.6 us (0.56)
  blocking collectives: 37.1 us -> 0 us
  Pallas kernels: 0 us -> 13.4 us
  matrix products: 10.1 us -> 0 us
  starting transfers between devices: 7.33 us -> 15.5 us
  waiting for transfers between devices: 16 us -> 10 us
  other arithmetic: 6.6 us -> 1.07 us
  local copies, waits for them, and re-layouts: 3.41 us -> 4.5 us
    psum x1 -> x0, blocking collectives: 37.1 us -> none  [on_device(): lax.psum((jnp.concatenate([surface_num, air_num[None, :]], axis=0), jnp.c...]
    all_to_all x1, waiting for transfers between devices: 16 us -> 0.01 us  [on_device(): lax.all_to_all(spread, ('comp', 'dom'), split_axis=0, concat_axis=0, tile...]
    pallas_call x0 -> x3, Pallas kernels: none -> 13.4 us  [the longest x1 9.64 us: on_device(): pl.pallas_call(remap_kernel, grid=(block_count // STEP_BLOCKS,), in_specs...]
    dot_general x2 -> x0, matrix products: 10.1 us -> none  [the longest x1 9.16 us: on_device(): jnp.einsum('fbs,btsa->btfa', blocks, remap_tiles, precision=lax.Precision...]
    ppermute x0 -> x7, waiting for transfers between devices: none -> 10 us  [the longest x6 8.34 us: exchange(): lax.ppermute(chunks[digit * part:(digit + 1) * part], 'dom', pairs)]
    ppermute x0 -> x7, starting transfers between devices: none -> 8.19 us  [the longest x6 7.94 us: exchange(): lax.ppermute(chunks[digit * part:(digit + 1) * part], 'dom', pairs)]
    reduce_sum x6 -> x0, other arithmetic: 4.45 us -> none  [the longest x1 1.52 us: on_device(): average = jnp.sum(surface_flux, axis=0) / step_count]
    all_to_all x1 -> x0, local copies, waits for them, and re-layouts: 1.41 us -> none  [on_device(): lax.all_to_all(outgoing, ('comp', 'dom'), split_axis=0, concat_axis=0, ti...]
  transfers between devices with their start and end apart: 1 -> 8, of which waited for: 1 -> 6; matrix products, arithmetic and copies ran while one was open for 3% -> 3% of each run, Pallas kernels for 0% -> 21%
where the time goes in v1:
time: 45.6 us; the launch traced here: 45.2 us
  starting transfers between devices  15.5 us (34%)
  Pallas kernels  13.4 us (29%)
  waiting for transfers between devices  10 us (22%)
  local copies, waits for them, and re-layouts  4.5 us (10%)
  other arithmetic  1.07 us (2%)
  between operations  0.68 us (1%)
    pallas_call x1, Pallas kernels, on_device(): pl.pallas_call(remap_kernel, grid=(block_count // STEP_BLOCKS,), in_specs...  9.64 us
    ppermute x6, waiting for transfers between devices, exchange(): lax.ppermute(chunks[digit * part:(digit + 1) * part], 'dom', pairs)  8.34 us
    ppermute x6, starting transfers between devices, exchange(): lax.ppermute(chunks[digit * part:(digit + 1) * part], 'dom', pairs)  7.94 us
    all_to_all x1, starting transfers between devices, on_device(): lax.all_to_all(spread, ('comp', 'dom'), split_axis=0, concat_axis=0, tile...  7.33 us
    pallas_call x1, Pallas kernels, on_device(): pl.pallas_call(functools.partial(weigh_kernel, order), in_specs=[vmem] *...  2.3 us
    ppermute x1, waiting for transfers between devices, on_device(): chunks = keep + lax.ppermute(send, 'comp', pairs)  1.68 us
    pallas_call x1, Pallas kernels, on_device(): pl.pallas_call(merge_kernel, in_specs=[vmem] * (len(pieces) + 3), out_spe...  1.48 us
    reshape x1, local copies, waits for them, and re-layouts, on_device(): air_row = air_area.reshape(1, air_cells)  1.26 us
  transfers between devices with their start and end apart: 8, of which 6 were waited for; matrix products, arithmetic and copies ran while one was open for 3% of the time, Pallas kernels for 21%

profile of v1, /device:TPU:0, one launch (start us, length us, event | category | flops | bytes accessed | tf_op | source)
XLA Modules:
  0.0 45.2 jit_solution(4599479599698210146)
XLA Ops:
  0.6 0.7 %slice.27 = f32[2,384]{1,0:T(2,128)S(1)} slice(f32[3,384]{1,0:T(4,128)} %refs_5_.1), slice={[0:2], [0:384]} | slice | bytes 6144 | tf_op jit(solution)/shard_map/slice | solution.py:168
  1.3 0.7 %broadcast_in_dim.9 = f32[32,1,384]{2,1,0:T(1,128)} reshape(f32[2,16,384]{2,1,0:T(8,128)S(1)} %broadcast_in_dim.8) | data formatting | bytes 98304 | tf_op jit(solution)/shard_map/broadcast_in_dim | solution.py:167
  2.0 7.3 %all-to-all-start = ((f32[32,1,384]{2,1,0:T(1,128)}), f32[32,1,384]{2,1,0:T(1,128)S(1)}, u32[]{:S(2)}, u32[]{:S(2)}) async-start(f32[32,1,384]{2,1,0:T(1,128)} %broadcast_in_dim.9), calls=%async_computation | async-start | bytes 98304 | tf_op jit(solution)/shard_map/all_to_all | solution.py:170
  9.3 1.3 %reshape.22.air_area.refs_6_ = f32[1,384]{1,0:T(1,128)} reshape(f32[384]{0:T(512)} %param.15) | data formatting | bytes 3072 | tf_op jit(solution)/shard_map/reshape | solution.py:165
  10.6 9.6 %remap.1 = (f32[32,16,384]{2,1,0:T(8,128)}, f32[16,128]{1,0:T(8,128)}) custom-call(s32[2,64]{1,0:T(2,128)} %bitcast.6, f32[6,12,4096]{2,1,0:T(8,128)} %flux.1, s32[32,128]{1,0:T(8,128)} %bitcast.5, f32[32,128]{1,0:T(8,128)} %bitcast.3, f32[64,2,64,384]{3,2,1,0:T(8,128)} %tiles.1), custom_call_target="tpu_custom_call" | custom-call | flops 603979776 | bytes 12582912 | tf_op jit(solution)/shard_map/remap/pallas_call | solution.py:173
  20.2 0.0 all-to-all-done.shares
  20.2 0.0 copy-start
  20.3 0.6 %copy-done = f32[32,1,384]{2,1,0:T(1,128)} copy-done((f32[32,1,384]{2,1,0:T(1,128)}, f32[32,1,384]{2,1,0:T(1,128)S(1)}, u32[]{:S(2)}) %copy-start) | copy-done | bytes 49176
  20.9 2.3 %weigh.1 = (f32[16,16,384]{2,1,0:T(8,128)}, f32[16,16,384]{2,1,0:T(8,128)}) custom-call(f32[32,16,384]{2,1,0:T(8,128)} %get-tuple-element.6.sums, f32[16,128]{1,0:T(8,128)} %get-tuple-element.7.weighted_sum, f32[32,1,384]{2,1,0:T(1,128)} %copy-done, f32[32,128]{1,0:T(8,128)} %bitcast.4, f32[12,384]{1,0:T(8,128)} %refs_4_.1, f32[3,384]{1,0:T(4,128)} %refs_5_.1, ...), custom_call_target="tpu_custom_call" | custom-call | tf_op jit(solution)/shard_map/weigh/pallas_call | solution.py:201
  23.2 0.3 collective-permute-start
  23.4 1.7 %collective-permute-done = f32[16,16,384]{2,1,0:T(8,128)S(1)} collective-permute-done((f32[16,16,384]{2,1,0:T(8,128)}, f32[16,16,384]{2,1,0:T(8,128)S(1)}, u32[]{:S(2)}, u32[]{:S(2)}) %collective-permute-start) | collective-permute-done | bytes 393248 | tf_op jit(solution)/shard_map/ppermute | solution.py:210
  25.1 1.0 %add.12 = f32[16,16,384]{2,1,0:T(8,128)S(1)} add(f32[16,16,384]{2,1,0:T(8,128)} %get-tuple-element.8, f32[16,16,384]{2,1,0:T(8,128)S(1)} %collective-permute-done) | non-fusion elementwise | flops 98304 | bytes 1179648 | tf_op jit(solution)/shard_map/add | solution.py:210
  26.2 2.7 %collective-permute-start.3 = (f32[4,16,384]{2,1,0:T(8,128)S(1)}, f32[4,16,384]{2,1,0:T(8,128)S(1)}, u32[]{:S(2)}, u32[]{:S(2)}) collective-permute-start(f32[4,16,384]{2,1,0:T(8,128)S(1)} %get-tuple-element.10), channel_id=1, source_target_pairs={{0,3},{1,2},{2,1},{3,0},{4,7},{5,6},{6,5},{7,4},{8,11},{9,10},{10,... | collective-permute-start | bytes 294920 | tf_op jit(solution)/shard_map/ppermute | solution.py:140
  28.9 0.6 %collective-permute-start.2 = (f32[4,16,384]{2,1,0:T(8,128)S(1)}, f32[4,16,384]{2,1,0:T(8,128)S(1)}, u32[]{:S(2)}, u32[]{:S(2)}) collective-permute-start(f32[4,16,384]{2,1,0:T(8,128)S(1)} %get-tuple-element.11), channel_id=1, source_target_pairs={{0,2},{1,3},{2,0},{3,1},{4,6},{5,7},{6,4},{7,5},{8,10},{9,11},{10,... | collective-permute-start | bytes 294920 | tf_op jit(solution)/shard_map/ppermute | solution.py:140
  29.5 0.3 collective-permute-start.1
  29.7 2.4 %collective-permute-done.3 = f32[4,16,384]{2,1,0:T(8,128)S(1)} collective-permute-done((f32[4,16,384]{2,1,0:T(8,128)S(1)}, f32[4,16,384]{2,1,0:T(8,128)S(1)}, u32[]{:S(2)}, u32[]{:S(2)}) %collective-permute-start.3) | collective-permute-done | bytes 98336 | tf_op jit(solution)/shard_map/ppermute | solution.py:140
  32.2 2.0 %collective-permute-done.2 = f32[4,16,384]{2,1,0:T(8,128)S(1)} collective-permute-done((f32[4,16,384]{2,1,0:T(8,128)S(1)}, f32[4,16,384]{2,1,0:T(8,128)S(1)}, u32[]{:S(2)}, u32[]{:S(2)}) %collective-permute-start.2) | collective-permute-done | bytes 98336 | tf_op jit(solution)/shard_map/ppermute | solution.py:140
  34.2 0.2 collective-permute-done.1
  34.4 0.6 %fusion.2 = (f32[1,16,384]{2,1,0:T(8,128)S(1)}, f32[1,16,384]{2,1,0:T(8,128)S(1)}, f32[1,16,384]{2,1,0:T(8,128)S(1)}, f32[1,16,384]{2,1,0:T(8,128)}) fusion(f32[4,16,384]{2,1,0:T(8,128)S(1)} %fusion), kind=kLoop, calls=%fused_computation.3 | loop fusion | bytes 196608 | tf_op jit(solution)/shard_map/slice | solution.py:140
  35.0 3.3 %collective-permute-start.6 = (f32[1,16,384]{2,1,0:T(8,128)S(1)}, f32[1,16,384]{2,1,0:T(8,128)S(1)}, u32[]{:S(2)}, u32[]{:S(2)}) collective-permute-start(f32[1,16,384]{2,1,0:T(8,128)S(1)} %get-tuple-element.13), channel_id=1, source_target_pairs={{0,12},{1,13},{2,14},{3,15},{4,8},{5,9},{6,10},{7,11},{8,4},{9,5},... | collective-permute-start | bytes 73736 | tf_op jit(solution)/shard_map/ppermute | solution.py:140
  38.4 0.0 collective-permute-start.5
  38.4 1.0 %collective-permute-start.4 = (f32[1,16,384]{2,1,0:T(8,128)S(1)}, f32[1,16,384]{2,1,0:T(8,128)S(1)}, u32[]{:S(2)}, u32[]{:S(2)}) collective-permute-start(f32[1,16,384]{2,1,0:T(8,128)S(1)} %get-tuple-element.15), channel_id=1, source_target_pairs={{0,4},{1,5},{2,6},{3,7},{4,0},{5,1},{6,2},{7,3},{8,12},{9,13},{10,... | collective-permute-start | bytes 73736 | tf_op jit(solution)/shard_map/ppermute | solution.py:140
  39.4 1.4 %collective-permute-done.6.refs_3_ = f32[1,16,384]{2,1,0:T(8,128)S(1)} collective-permute-done((f32[1,16,384]{2,1,0:T(8,128)S(1)}, f32[1,16,384]{2,1,0:T(8,128)S(1)}, u32[]{:S(2)}, u32[]{:S(2)}) %collective-permute-start.6) | collective-permute-done | bytes 24608 | tf_op jit(solution)/shard_map/ppermute | solution.py:140
  40.8 0.0 copy-start.1
  40.8 2.3 %collective-permute-done.5.refs_2_ = f32[1,16,384]{2,1,0:T(8,128)S(1)} collective-permute-done((f32[1,16,384]{2,1,0:T(8,128)S(1)}, f32[1,16,384]{2,1,0:T(8,128)S(1)}, u32[]{:S(2)}, u32[]{:S(2)}) %collective-permute-start.5) | collective-permute-done | bytes 24608 | tf_op jit(solution)/shard_map/ppermute | solution.py:140
  43.1 0.0 copy-start.2
  43.1 0.0 collective-permute-done.4.refs_1_
  43.1 0.0 copy-start.3
  43.1 0.0 copy-done.1
  43.1 0.6 %copy-done.2 = f32[1,16,384]{2,1,0:T(8,128)} copy-done((f32[1,16,384]{2,1,0:T(8,128)}, f32[1,16,384]{2,1,0:T(8,128)S(1)}, u32[]{:S(2)}) %copy-start.2) | copy-done | bytes 24600
  43.7 0.0 copy-done.3
  43.7 1.5 %merge.1 = (f32[12,384]{1,0:T(8,128)}, f32[3,12]{1,0:T(4,128)}) custom-call(f32[1,16,384]{2,1,0:T(8,128)} %get-tuple-element.16.refs_0_, f32[1,16,384]{2,1,0:T(8,128)} %copy-done.3, f32[1,16,384]{2,1,0:T(8,128)} %copy-done.2, f32[1,16,384]{2,1,0:T(8,128)} %copy-done.1, f32[12,384]{1,0:T(8,128)} %refs_4_.1, f32[3,384]{1,0:T(4,128)} %refs_5_.1, ...), custom_call_target="tpu_custom_call" | custom-call | tf_op jit(solution)/shard_map/merge/pallas_call | solution.py:215
  (3 shorter events, 0.1 us)
Async XLA Ops:
  2.0 18.2 %all-to-all-start = ((f32[32,1,384]{2,1,0:T(1,128)}), f32[32,1,384]{2,1,0:T(1,128)S(1)}, u32[]{:S(2)}, u32[]{:S(2)}) async-start(f32[32,1,384]{2,1,0:T(1,128)} %broadcast_in_dim.9), calls=%async_computation | async-start | bytes 98304 | tf_op jit(solution)/shard_map/all_to_all | solution.py:170
  20.2 0.6 %copy-start = (f32[32,1,384]{2,1,0:T(1,128)}, f32[32,1,384]{2,1,0:T(1,128)S(1)}, u32[]{:S(2)}) copy-start(f32[32,1,384]{2,1,0:T(1,128)S(1)} %all-to-all-done.shares) | copy-start | bytes 147460
  23.2 1.9 %collective-permute-start = (f32[16,16,384]{2,1,0:T(8,128)}, f32[16,16,384]{2,1,0:T(8,128)S(1)}, u32[]{:S(2)}, u32[]{:S(2)}) collective-permute-start(f32[16,16,384]{2,1,0:T(8,128)} %get-tuple-element.9), channel_id=1, source_target_pairs={{0,16},{16,0},{1,17},{17,1},{2,18},{18,2},{3,19},{19,3},{4,20},{20... | collective-permute-start | bytes 1179656 | tf_op jit(solution)/shard_map/ppermute | solution.py:210
  26.2 6.0 %collective-permute-start.3 = (f32[4,16,384]{2,1,0:T(8,128)S(1)}, f32[4,16,384]{2,1,0:T(8,128)S(1)}, u32[]{:S(2)}, u32[]{:S(2)}) collective-permute-start(f32[4,16,384]{2,1,0:T(8,128)S(1)} %get-tuple-element.10), channel_id=1, source_target_pairs={{0,3},{1,2},{2,1},{3,0},{4,7},{5,6},{6,5},{7,4},{8,11},{9,10},{10,... | collective-permute-start | bytes 294920 | tf_op jit(solution)/shard_map/ppermute | solution.py:140
  28.9 5.3 %collective-permute-start.2 = (f32[4,16,384]{2,1,0:T(8,128)S(1)}, f32[4,16,384]{2,1,0:T(8,128)S(1)}, u32[]{:S(2)}, u32[]{:S(2)}) collective-permute-start(f32[4,16,384]{2,1,0:T(8,128)S(1)} %get-tuple-element.11), channel_id=1, source_target_pairs={{0,2},{1,3},{2,0},{3,1},{4,6},{5,7},{6,4},{7,5},{8,10},{9,11},{10,... | collective-permute-start | bytes 294920 | tf_op jit(solution)/shard_map/ppermute | solution.py:140
  29.5 4.9 %collective-permute-start.1 = (f32[4,16,384]{2,1,0:T(8,128)S(1)}, f32[4,16,384]{2,1,0:T(8,128)S(1)}, u32[]{:S(2)}, u32[]{:S(2)}) collective-permute-start(f32[4,16,384]{2,1,0:T(8,128)S(1)} %get-tuple-element.12), channel_id=1, source_target_pairs={{0,1},{1,0},{2,3},{3,2},{4,5},{5,4},{6,7},{7,6},{8,9},{9,8},{10,11... | collective-permute-start | bytes 294920 | tf_op jit(solution)/shard_map/ppermute | solution.py:140
  35.0 5.8 %collective-permute-start.6 = (f32[1,16,384]{2,1,0:T(8,128)S(1)}, f32[1,16,384]{2,1,0:T(8,128)S(1)}, u32[]{:S(2)}, u32[]{:S(2)}) collective-permute-start(f32[1,16,384]{2,1,0:T(8,128)S(1)} %get-tuple-element.13), channel_id=1, source_target_pairs={{0,12},{1,13},{2,14},{3,15},{4,8},{5,9},{6,10},{7,11},{8,4},{9,5},... | collective-permute-start | bytes 73736 | tf_op jit(solution)/shard_map/ppermute | solution.py:140
  38.4 4.7 %collective-permute-start.5 = (f32[1,16,384]{2,1,0:T(8,128)S(1)}, f32[1,16,384]{2,1,0:T(8,128)S(1)}, u32[]{:S(2)}, u32[]{:S(2)}) collective-permute-start(f32[1,16,384]{2,1,0:T(8,128)S(1)} %get-tuple-element.14), channel_id=1, source_target_pairs={{0,8},{1,9},{2,10},{3,11},{4,12},{5,13},{6,14},{7,15},{8,0},{9,1},... | collective-permute-start | bytes 73736 | tf_op jit(solution)/shard_map/ppermute | solution.py:140
  38.4 4.7 %collective-permute-start.4 = (f32[1,16,384]{2,1,0:T(8,128)S(1)}, f32[1,16,384]{2,1,0:T(8,128)S(1)}, u32[]{:S(2)}, u32[]{:S(2)}) collective-permute-start(f32[1,16,384]{2,1,0:T(8,128)S(1)} %get-tuple-element.15), channel_id=1, source_target_pairs={{0,4},{1,5},{2,6},{3,7},{4,0},{5,1},{6,2},{7,3},{8,12},{9,13},{10,... | collective-permute-start | bytes 73736 | tf_op jit(solution)/shard_map/ppermute | solution.py:140
  40.8 2.3 %copy-start.1 = (f32[1,16,384]{2,1,0:T(8,128)}, f32[1,16,384]{2,1,0:T(8,128)S(1)}, u32[]{:S(2)}) copy-start(f32[1,16,384]{2,1,0:T(8,128)S(1)} %collective-permute-done.6.refs_3_) | copy-start | bytes 73732
  43.1 0.6 %copy-start.2 = (f32[1,16,384]{2,1,0:T(8,128)}, f32[1,16,384]{2,1,0:T(8,128)S(1)}, u32[]{:S(2)}) copy-start(f32[1,16,384]{2,1,0:T(8,128)S(1)} %collective-permute-done.5.refs_2_) | copy-start | bytes 73732
  43.1 0.6 %copy-start.3 = (f32[1,16,384]{2,1,0:T(8,128)}, f32[1,16,384]{2,1,0:T(8,128)S(1)}, u32[]{:S(2)}) copy-start(f32[1,16,384]{2,1,0:T(8,128)S(1)} %collective-permute-done.4.refs_1_) | copy-start | bytes 73732

commit v2 on v1

v2 whole, which is shorter than its diff:
```python
import functools

import jax
import jax.numpy as jnp
from jax import lax
from jax.experimental import pallas as pl
from jax.experimental.pallas import tpu as pltpu
from jax.sharding import PartitionSpec as P

QUAD = 4
STEP_BLOCKS = 8
ROWS = 16


def split(x):
    hi = x.astype(jnp.bfloat16)
    lo = (x - hi.astype(jnp.float32)).astype(jnp.bfloat16)
    return hi, lo


def own_position():
    return lax.axis_index("comp") * lax.axis_size("dom") + lax.axis_index("dom")


def phase_plan(domain_count):
    plan, stride = [], 1
    while stride < domain_count:
        radix = 4 if domain_count // stride >= 4 else 2
        plan.append((radix, stride))
        stride *= radix
    return plan


def chunk_order(domain_count):
    order = [0]
    for radix, stride in reversed(phase_plan(domain_count)):
        order = [digit * stride + rest for digit in range(radix) for rest in order]
    return order


def remap_kernel(
    targets, flux_hbm, mask, area, tiles_hbm, sums, weighted_sum, flux, tiles, arrived, padded
):
    me = own_position()
    chunk_count, step_count, field_count, step_cells = flux.shape
    _, intersection, block_cells, air_cells = tiles_hbm.shape
    cells = QUAD * block_cells
    lanes = mask.shape[1]

    def copies(chunk):
        cell = chunk * step_cells
        block = chunk * STEP_BLOCKS
        return (
            pltpu.make_async_copy(
                flux_hbm.at[:, :, pl.ds(cell, step_cells)], flux.at[chunk], arrived.at[0, chunk]
            ),
            pltpu.make_async_copy(
                tiles_hbm.at[pl.ds(block, STEP_BLOCKS)],
                tiles.at[pl.ds(block, STEP_BLOCKS)],
                arrived.at[1, chunk],
            ),
        )

    for chunk in range(chunk_count):
        for copy in copies(chunk):
            copy.start()

    sums[...] = jnp.zeros_like(sums)
    weighted_sum[...] = jnp.zeros_like(weighted_sum)
    padded[...] = jnp.zeros_like(padded)
    row_block = lax.broadcasted_iota(jnp.int32, (QUAD * ROWS, cells), 0) // ROWS
    col_block = lax.broadcasted_iota(jnp.int32, (QUAD * ROWS, cells), 1) // block_cells
    diagonal = row_block == col_block

    @pl.loop(0, chunk_count)
    def _(chunk):
        for copy in copies(chunk):
            copy.wait()
        for quad in range(STEP_BLOCKS // QUAD):
            for part in range(cells // lanes):
                start = quad * cells + part * lanes
                row = chunk * (step_cells // lanes) + start // lanes
                total = flux[chunk, 0, :, start : start + lanes]
                for s in range(1, step_count):
                    total = total + flux[chunk, s, :, start : start + lanes]
                coverage = mask[pl.ds(row, 1), :].astype(jnp.float32) * area[pl.ds(row, 1), :]
                weighted = (total / step_count) * coverage
                weighted_sum[0:field_count, :] += weighted
                padded[quad, 0:field_count, part * lanes : (part + 1) * lanes] = weighted
            value = padded[quad]
            left = jnp.where(diagonal, jnp.concatenate([value] * QUAD, axis=0), 0.0)
            left_hi, left_lo = split(left)
            left_both = jnp.concatenate([left_hi, left_lo], axis=0)
            first_block = chunk * STEP_BLOCKS + quad * QUAD
            for slot in range(intersection):
                right = tiles[pl.ds(first_block, QUAD), slot].reshape(cells, air_cells)
                right_hi, right_lo = split(right)
                first = jnp.dot(left_both, right_hi, preferred_element_type=jnp.float32)
                second = jnp.dot(left_hi, right_lo, preferred_element_type=jnp.float32)
                made = first[: QUAD * ROWS] + (first[QUAD * ROWS :] + second)
                for b in range(QUAD):
                    sums[targets[slot, first_block + b] ^ me] += made[b * ROWS : (b + 1) * ROWS]


def as_row(column, width):
    eye = lax.broadcasted_iota(jnp.int32, (column.shape[0], width), 0) == lax.broadcasted_iota(
        jnp.int32, (column.shape[0], width), 1
    )
    return jnp.sum(jnp.where(eye, column, 0.0), axis=0, keepdims=True)


def weigh_kernel(order, sums, weighted_sum, shares, area, ocean, fraction, air_area, keep, send):
    me = own_position()
    own_group = lax.axis_index("comp")
    domain_count = len(order)
    field_count, width = ocean.shape
    air_row = air_area[...][None, :]
    total = jnp.zeros(sums.shape[1:], jnp.float32)
    for owner in range(2 * domain_count):
        total = total + sums[owner] * shares[owner ^ me]
    ocean_term = fraction[2:3, :] * ocean[...] * air_row
    air_num = as_row(jnp.sum(total, axis=1, keepdims=True), width) + as_row(
        jnp.sum(ocean_term, axis=1, keepdims=True), width
    )
    air_den = jnp.sum(air_row)
    surface_num = as_row(jnp.sum(weighted_sum[...], axis=1, keepdims=True), width)
    surface_den = jnp.sum(area[...])
    lane = lax.broadcasted_iota(jnp.int32, (1, width), 1)
    surface = jnp.where(lane == field_count, surface_den, surface_num)
    air = jnp.where(lane == field_count, air_den, air_num)
    row = lax.broadcasted_iota(jnp.int32, (ROWS, width), 0)
    extra = jnp.where(row == field_count + own_group, surface, 0.0)
    extra = jnp.where(row == field_count + 2, air, extra)
    for slot, place in enumerate(order):
        keep[slot] = sums[place] * shares[place ^ me] + extra
        far = domain_count + place
        send[slot] = sums[far] * shares[far ^ me] + extra


def tree_sum(items):
    while len(items) > 1:
        items = [items[i] + items[i + 1] for i in range(0, len(items), 2)]
    return items[0]


def cut(chunks, radix):
    part = chunks.shape[0] // radix
    return [chunks[digit * part : (digit + 1) * part] for digit in range(radix)]


def exchange(parts, stride):
    domain_count = lax.axis_size("dom")
    pieces = [parts[0]]
    for digit in range(1, len(parts)):
        pairs = [(i, i ^ (digit * stride)) for i in range(domain_count)]
        pieces.append(lax.ppermute(parts[digit], "dom", pairs))
    return pieces


def on_device(
    surface_flux,
    active_mask,
    source_area,
    tile_targets,
    remap_tiles,
    ocean_flux,
    air_fraction,
    air_area,
):
    step_count, field_count, cell_count = surface_flux.shape
    block_count, intersection, block_cells, air_cells = remap_tiles.shape
    group_count = lax.axis_size("comp")
    domain_count = lax.axis_size("dom")
    owner_count = group_count * domain_count
    lanes = 128
    order = chunk_order(domain_count)
    vmem = pl.BlockSpec(memory_space=pltpu.VMEM)

    mask = active_mask.reshape(cell_count // lanes, lanes)
    area = source_area.reshape(cell_count // lanes, lanes)

    spread = jnp.broadcast_to(
        air_fraction[:group_count, None, None, :], (group_count, domain_count, 1, air_cells)
    ).reshape(owner_count, 1, air_cells)
    shares = lax.all_to_all(spread, ("comp", "dom"), split_axis=0, concat_axis=0, tiled=True)

    step_cells = STEP_BLOCKS * block_cells
    chunk_count = block_count // STEP_BLOCKS
    half = jax.ShapeDtypeStruct((domain_count, ROWS, air_cells), jnp.float32)
    sums, weighted_sum = pl.pallas_call(
        remap_kernel,
        in_specs=[
            pl.BlockSpec(memory_space=pltpu.SMEM),
            pl.BlockSpec(memory_space=pl.ANY),
            vmem,
            vmem,
            pl.BlockSpec(memory_space=pl.ANY),
        ],
        out_specs=[vmem] * 2,
        out_shape=[
            jax.ShapeDtypeStruct((owner_count, ROWS, air_cells), jnp.float32),
            jax.ShapeDtypeStruct((ROWS, lanes), jnp.float32),
        ],
        scratch_shapes=[
            pltpu.VMEM((chunk_count, step_count, field_count, step_cells), jnp.float32),
            pltpu.VMEM(remap_tiles.shape, jnp.float32),
            pltpu.SemaphoreType.DMA((2, chunk_count)),
            pltpu.VMEM((STEP_BLOCKS // QUAD, ROWS, QUAD * block_cells), jnp.float32),
        ],
        cost_estimate=pl.CostEstimate(
            flops=2 * 16 * 6 * remap_tiles.size, bytes_accessed=4 * remap_tiles.size, transcendentals=0
        ),
        name="remap",
    )(tile_targets.T, surface_flux, mask, area, remap_tiles)

    keep, send = pl.pallas_call(
        functools.partial(weigh_kernel, order),
        in_specs=[vmem] * 7,
        out_specs=[vmem] * 2,
        out_shape=[half, half],
        name="weigh",
    )(sums, weighted_sum, shares, area, ocean_flux, air_fraction, air_area)

    pairs = [(i, i ^ 1) for i in range(group_count)]
    pieces = [keep, lax.ppermute(send, "comp", pairs)]
    for radix, stride in phase_plan(domain_count):
        pieces = exchange(cut(tree_sum(pieces), radix), stride)
    total = tree_sum(pieces)[0]
    merged = total[:field_count] / air_area[None, :] + air_fraction[2][None, :] * ocean_flux
    rows = total[field_count : field_count + group_count + 1]
    means = rows[:, :field_count] / rows[:, field_count : field_count + 1]
    return (merged, means)


def solution(mesh):
    in_specs = (
        P(None, None, ("comp", "dom")),
        P(("comp", "dom")),
        P(("comp", "dom")),
        P(("comp", "dom"), None),
        P(("comp", "dom"), None, None, None),
        P(None, ("comp", "dom")),
        P(None, ("comp", "dom")),
        P(("comp", "dom")),
    )
    out_specs = (P(None, ("comp", "dom")), P())
    return jax.shard_map(
        on_device, mesh=mesh, in_specs=in_specs, out_specs=out_specs, check_vma=False
    )
```

time: 45.6 us -> 43 us (0.943)
  Pallas kernels: 13.4 us -> 9.61 us
  local copies, waits for them, and re-layouts: 4.5 us -> 2.94 us
  waiting for transfers between devices: 10 us -> 11.4 us
  other arithmetic: 1.07 us -> 2.36 us
    pallas_call x2 -> x1, Pallas kernels: 11.1 us -> 7.31 us  [on_device(): pl.pallas_call(remap_kernel, in_specs=[pl.BlockSpec(memory_space=pltpu.SM...]
    ppermute x7, waiting for transfers between devices: 10 us -> 11.4 us  [the longest x6 9.71 us: exchange(): pieces.append(lax.ppermute(parts[digit], 'dom', pairs))]
    reshape x1 -> x0, local copies, waits for them, and re-layouts: 1.26 us -> none  [on_device(): air_row = air_area.reshape(1, air_cells)]
    add x1 -> x3, other arithmetic: 0.02 us -> 1.08 us  [tree_sum(): items = [items[i] + items[i + 1] for i in range(0, len(items), 2)]]
    div x0 -> x1, other arithmetic: none -> 0.66 us  [on_device(): means = rows[:, :field_count] / rows[:, field_count:field_count + 1]]
    unnamed x8 -> x6, local copies, waits for them, and re-layouts: 1.23 us -> 0.62 us
    slice x2 -> x5, local copies, waits for them, and re-layouts: 0.64 us -> 0.93 us  [the longest x1 0.71 us: on_device(): air_fraction[2][None, :] * ocean_flux]
  transfers between devices with their start and end apart: 8 -> 8, of which waited for: 6 -> 6; matrix products, arithmetic and copies ran while one was open for 3% -> 2% of each run, Pallas kernels for 21% -> 17%
where the time goes in v2:
time: 43 us; the launch traced here: 42.6 us
  starting transfers between devices  15.6 us (36%)
  waiting for transfers between devices  11.4 us (27%)
  Pallas kernels  9.61 us (22%)
  local copies, waits for them, and re-layouts  2.94 us (7%)
  other arithmetic  2.36 us (5%)
  between operations  0.72 us (2%)
    ppermute x6, waiting for transfers between devices, exchange(): pieces.append(lax.ppermute(parts[digit], 'dom', pairs))  9.71 us
    ppermute x6, starting transfers between devices, exchange(): pieces.append(lax.ppermute(parts[digit], 'dom', pairs))  8.01 us
    all_to_all x1, starting transfers between devices, on_device(): lax.all_to_all(spread, ('comp', 'dom'), split_axis=0, concat_axis=0, tile...  7.33 us
    pallas_call x1, Pallas kernels, on_device(): pl.pallas_call(remap_kernel, in_specs=[pl.BlockSpec(memory_space=pltpu.SM...  7.31 us
    pallas_call x1, Pallas kernels, on_device(): pl.pallas_call(functools.partial(weigh_kernel, order), in_specs=[vmem] *...  2.3 us
    ppermute x1, waiting for transfers between devices, on_device(): pieces = [keep, lax.ppermute(send, 'comp', pairs)]  1.68 us
    add x3, other arithmetic, tree_sum(): items = [items[i] + items[i + 1] for i in range(0, len(items), 2)]  1.08 us
  transfers between devices with their start and end apart: 8, of which 6 were waited for; matrix products, arithmetic and copies ran while one was open for 2% of the time, Pallas kernels for 17%

profile of v2, /device:TPU:0, one launch (start us, length us, event | category | flops | bytes accessed | tf_op | source)
XLA Modules:
  0.0 42.6 jit_solution(8000984686923356690)
XLA Ops:
  0.6 0.0 copy-start.1
  0.6 0.0 copy-start.2
  0.7 0.7 %slice.48 = f32[2,384]{1,0:T(2,128)S(1)} slice(f32[3,384]{1,0:T(4,128)} %fraction.1), slice={[0:2], [0:384]} | slice | bytes 6144 | tf_op jit(solution)/shard_map/slice | solution.py:183
  1.4 0.7 %broadcast_in_dim.10 = f32[32,1,384]{2,1,0:T(1,128)} reshape(f32[2,16,384]{2,1,0:T(8,128)S(1)} %broadcast_in_dim.4) | data formatting | bytes 98304 | tf_op jit(solution)/shard_map/broadcast_in_dim | solution.py:182
  2.0 7.3 %all-to-all-start = ((f32[32,1,384]{2,1,0:T(1,128)}), f32[32,1,384]{2,1,0:T(1,128)S(1)}, u32[]{:S(2)}, u32[]{:S(2)}) async-start(f32[32,1,384]{2,1,0:T(1,128)} %broadcast_in_dim.10), calls=%async_computation | async-start | bytes 98304 | tf_op jit(solution)/shard_map/all_to_all | solution.py:185
  9.4 7.3 %remap.1 = (f32[32,16,384]{2,1,0:T(8,128)}, f32[16,128]{1,0:T(8,128)}) custom-call(s32[2,64]{1,0:T(2,128)} %bitcast.14, f32[6,12,4096]{2,1,0:T(8,128)} %flux_hbm.1, s32[32,128]{1,0:T(8,128)} %bitcast.13, f32[32,128]{1,0:T(8,128)} %bitcast.11, f32[64,2,64,384]{3,2,1,0:T(8,128)} %tiles_hbm.1), custom_call_target="tpu_custom_call" | custom-call | flops 603979776 | bytes 12582912 | tf_op jit(solution)/shard_map/remap/pallas_call | solution.py:190
  16.7 0.0 all-to-all-done.shares
  16.7 0.0 copy-start
  16.7 0.6 %copy-done = f32[32,1,384]{2,1,0:T(1,128)} copy-done((f32[32,1,384]{2,1,0:T(1,128)}, f32[32,1,384]{2,1,0:T(1,128)S(1)}, u32[]{:S(2)}) %copy-start) | copy-done | bytes 49176
  17.3 2.3 %weigh.1 = (f32[16,16,384]{2,1,0:T(8,128)}, f32[16,16,384]{2,1,0:T(8,128)}) custom-call(f32[32,16,384]{2,1,0:T(8,128)} %get-tuple-element.6.sums, f32[16,128]{1,0:T(8,128)} %get-tuple-element.7.weighted_sum, f32[32,1,384]{2,1,0:T(1,128)} %copy-done, f32[32,128]{1,0:T(8,128)} %bitcast.12, f32[12,384]{1,0:T(8,128)} %ocean.1, f32[3,384]{1,0:T(4,128)} %fraction.1, ...), custom_call_target="tpu_custom_call" | custom-call | tf_op jit(solution)/shard_map/weigh/pallas_call | solution.py:216
  19.6 0.3 collective-permute-start
  19.9 1.7 %collective-permute-done = f32[16,16,384]{2,1,0:T(8,128)S(1)} collective-permute-done((f32[16,16,384]{2,1,0:T(8,128)}, f32[16,16,384]{2,1,0:T(8,128)S(1)}, u32[]{:S(2)}, u32[]{:S(2)}) %collective-permute-start) | collective-permute-done | bytes 393248 | tf_op jit(solution)/shard_map/ppermute | solution.py:225
  21.6 1.0 %add.24 = f32[16,16,384]{2,1,0:T(8,128)S(1)} add(f32[16,16,384]{2,1,0:T(8,128)} %get-tuple-element.8, f32[16,16,384]{2,1,0:T(8,128)S(1)} %collective-permute-done) | non-fusion elementwise | flops 98304 | bytes 1179648 | tf_op jit(solution)/shard_map/add | solution.py:142
  22.6 1.8 %collective-permute-start.1 = (f32[4,16,384]{2,1,0:T(8,128)S(1)}, f32[4,16,384]{2,1,0:T(8,128)S(1)}, u32[]{:S(2)}, u32[]{:S(2)}) collective-permute-start(f32[4,16,384]{2,1,0:T(8,128)S(1)} %get-tuple-element.12), channel_id=1, source_target_pairs={{0,1},{1,0},{2,3},{3,2},{4,5},{5,4},{6,7},{7,6},{8,9},{9,8},{10,11... | collective-permute-start | bytes 294920 | tf_op jit(solution)/shard_map/ppermute | solution.py:156
  24.5 1.5 %collective-permute-start.2 = (f32[4,16,384]{2,1,0:T(8,128)S(1)}, f32[4,16,384]{2,1,0:T(8,128)S(1)}, u32[]{:S(2)}, u32[]{:S(2)}) collective-permute-start(f32[4,16,384]{2,1,0:T(8,128)S(1)} %get-tuple-element.11), channel_id=1, source_target_pairs={{0,2},{1,3},{2,0},{3,1},{4,6},{5,7},{6,4},{7,5},{8,10},{9,11},{10,... | collective-permute-start | bytes 294920 | tf_op jit(solution)/shard_map/ppermute | solution.py:156
  25.9 0.2 collective-permute-start.3
  26.2 1.5 %collective-permute-done.1 = f32[4,16,384]{2,1,0:T(8,128)S(1)} collective-permute-done((f32[4,16,384]{2,1,0:T(8,128)S(1)}, f32[4,16,384]{2,1,0:T(8,128)S(1)}, u32[]{:S(2)}, u32[]{:S(2)}) %collective-permute-start.1) | collective-permute-done | bytes 98336 | tf_op jit(solution)/shard_map/ppermute | solution.py:156
  27.7 2.5 %collective-permute-done.2 = f32[4,16,384]{2,1,0:T(8,128)S(1)} collective-permute-done((f32[4,16,384]{2,1,0:T(8,128)S(1)}, f32[4,16,384]{2,1,0:T(8,128)S(1)}, u32[]{:S(2)}, u32[]{:S(2)}) %collective-permute-start.2) | collective-permute-done | bytes 98336 | tf_op jit(solution)/shard_map/ppermute | solution.py:156
  30.2 1.3 %collective-permute-done.3 = f32[4,16,384]{2,1,0:T(8,128)S(1)} collective-permute-done((f32[4,16,384]{2,1,0:T(8,128)S(1)}, f32[4,16,384]{2,1,0:T(8,128)S(1)}, u32[]{:S(2)}, u32[]{:S(2)}) %collective-permute-start.3) | collective-permute-done | bytes 98336 | tf_op jit(solution)/shard_map/ppermute | solution.py:156
  31.5 1.5 %collective-permute-start.4 = (f32[1,16,384]{2,1,0:T(8,128)S(1)}, f32[1,16,384]{2,1,0:T(8,128)S(1)}, u32[]{:S(2)}, u32[]{:S(2)}) collective-permute-start(f32[1,16,384]{2,1,0:T(8,128)S(1)} %get-tuple-element.15), channel_id=1, source_target_pairs={{0,4},{1,5},{2,6},{3,7},{4,0},{5,1},{6,2},{7,3},{8,12},{9,13},{10,... | collective-permute-start | bytes 73736 | tf_op jit(solution)/shard_map/ppermute | solution.py:156
  33.0 2.5 %collective-permute-start.5 = (f32[1,16,384]{2,1,0:T(8,128)S(1)}, f32[1,16,384]{2,1,0:T(8,128)S(1)}, u32[]{:S(2)}, u32[]{:S(2)}) collective-permute-start(f32[1,16,384]{2,1,0:T(8,128)S(1)} %get-tuple-element.14), channel_id=1, source_target_pairs={{0,8},{1,9},{2,10},{3,11},{4,12},{5,13},{6,14},{7,15},{8,0},{9,1},... | collective-permute-start | bytes 73736 | tf_op jit(solution)/shard_map/ppermute | solution.py:156
  35.5 0.5 %collective-permute-start.6 = (f32[1,16,384]{2,1,0:T(8,128)S(1)}, f32[1,16,384]{2,1,0:T(8,128)S(1)}, u32[]{:S(2)}, u32[]{:S(2)}) collective-permute-start(f32[1,16,384]{2,1,0:T(8,128)S(1)} %get-tuple-element.13), channel_id=1, source_target_pairs={{0,12},{1,13},{2,14},{3,15},{4,8},{5,9},{6,10},{7,11},{8,4},{9,5},... | collective-permute-start | bytes 73736 | tf_op jit(solution)/shard_map/ppermute | solution.py:156
  36.0 0.7 %slice_reduce_fusion.1 = f32[384]{0:T(512)S(1)} fusion(f32[3,384]{1,0:T(4,128)} %fraction.1), kind=kLoop, calls=%fused_computation.10 | loop fusion | bytes 3072 | tf_op jit(solution)/shard_map/slice | solution.py:229
  36.7 0.0 collective-permute-done.4
  36.7 1.6 %collective-permute-done.5 = f32[1,16,384]{2,1,0:T(8,128)S(1)} collective-permute-done((f32[1,16,384]{2,1,0:T(8,128)S(1)}, f32[1,16,384]{2,1,0:T(8,128)S(1)}, u32[]{:S(2)}, u32[]{:S(2)}) %collective-permute-start.5) | collective-permute-done | bytes 24608 | tf_op jit(solution)/shard_map/ppermute | solution.py:156
  38.3 2.8 %collective-permute-done.6 = f32[1,16,384]{2,1,0:T(8,128)S(1)} collective-permute-done((f32[1,16,384]{2,1,0:T(8,128)S(1)}, f32[1,16,384]{2,1,0:T(8,128)S(1)}, u32[]{:S(2)}, u32[]{:S(2)}) %collective-permute-start.6) | collective-permute-done | bytes 24608 | tf_op jit(solution)/shard_map/ppermute | solution.py:156
  41.1 0.2 slice_reduce_fusion
  41.3 0.7 %slice_divide_fusion = f32[3,12]{1,0:T(4,128)} fusion(f32[3,384]{1,0:T(4,128)S(1)} %slice_bitcast_fusion.1, f32[3]{0:T(128)S(1)} %slice_reduce_fusion), kind=kLoop, calls=%fused_computation.9 | loop fusion | flops 36 | bytes 300 | tf_op jit(solution)/shard_map/div | solution.py:231
  42.0 0.0 copy-done.1
  42.0 0.0 copy-done.2
  42.0 0.6 %fusion.2 = f32[12,384]{1,0:T(8,128)} fusion(f32[1,16,384]{2,1,0:T(8,128)S(1)} %fusion.3, f32[12,384]{1,0:T(8,128)S(1)} %copy-done.1, f32[384]{0:T(512)S(1)} %slice_reduce_fusion.1, f32[384]{0:T(512)S(1)} %copy-done.2), kind=kLoop, calls=%fused_computation.4 | loop fusion | flops 13824 | bytes 58368 | tf_op jit(solution)/shard_map/add | solution.py:229
  (6 shorter events, 0.1 us)
Async XLA Ops:
  0.6 41.4 %copy-start.1 = (f32[12,384]{1,0:T(8,128)S(1)}, f32[12,384]{1,0:T(8,128)}, u32[]{:S(2)}) copy-start(f32[12,384]{1,0:T(8,128)} %ocean.1) | copy-start | bytes 55300
  0.6 41.4 %copy-start.2 = (f32[384]{0:T(512)S(1)}, f32[384]{0:T(512)}, u32[]{:S(2)}) copy-start(f32[384]{0:T(512)} %air_area.1) | copy-start | bytes 4612
  2.0 14.7 %all-to-all-start = ((f32[32,1,384]{2,1,0:T(1,128)}), f32[32,1,384]{2,1,0:T(1,128)S(1)}, u32[]{:S(2)}, u32[]{:S(2)}) async-start(f32[32,1,384]{2,1,0:T(1,128)} %broadcast_in_dim.10), calls=%async_computation | async-start | bytes 98304 | tf_op jit(solution)/shard_map/all_to_all | solution.py:185
  16.7 0.6 %copy-start = (f32[32,1,384]{2,1,0:T(1,128)}, f32[32,1,384]{2,1,0:T(1,128)S(1)}, u32[]{:S(2)}) copy-start(f32[32,1,384]{2,1,0:T(1,128)S(1)} %all-to-all-done.shares) | copy-start | bytes 147460
  19.6 1.9 %collective-permute-start = (f32[16,16,384]{2,1,0:T(8,128)}, f32[16,16,384]{2,1,0:T(8,128)S(1)}, u32[]{:S(2)}, u32[]{:S(2)}) collective-permute-start(f32[16,16,384]{2,1,0:T(8,128)} %get-tuple-element.9), channel_id=1, source_target_pairs={{0,16},{16,0},{1,17},{17,1},{2,18},{18,2},{3,19},{19,3},{4,20},{20... | collective-permute-start | bytes 1179656 | tf_op jit(solution)/shard_map/ppermute | solution.py:225
  22.6 5.0 %collective-permute-start.1 = (f32[4,16,384]{2,1,0:T(8,128)S(1)}, f32[4,16,384]{2,1,0:T(8,128)S(1)}, u32[]{:S(2)}, u32[]{:S(2)}) collective-permute-start(f32[4,16,384]{2,1,0:T(8,128)S(1)} %get-tuple-element.12), channel_id=1, source_target_pairs={{0,1},{1,0},{2,3},{3,2},{4,5},{5,4},{6,7},{7,6},{8,9},{9,8},{10,11... | collective-permute-start | bytes 294920 | tf_op jit(solution)/shard_map/ppermute | solution.py:156
  24.5 5.7 %collective-permute-start.2 = (f32[4,16,384]{2,1,0:T(8,128)S(1)}, f32[4,16,384]{2,1,0:T(8,128)S(1)}, u32[]{:S(2)}, u32[]{:S(2)}) collective-permute-start(f32[4,16,384]{2,1,0:T(8,128)S(1)} %get-tuple-element.11), channel_id=1, source_target_pairs={{0,2},{1,3},{2,0},{3,1},{4,6},{5,7},{6,4},{7,5},{8,10},{9,11},{10,... | collective-permute-start | bytes 294920 | tf_op jit(solution)/shard_map/ppermute | solution.py:156
  25.9 5.5 %collective-permute-start.3 = (f32[4,16,384]{2,1,0:T(8,128)S(1)}, f32[4,16,384]{2,1,0:T(8,128)S(1)}, u32[]{:S(2)}, u32[]{:S(2)}) collective-permute-start(f32[4,16,384]{2,1,0:T(8,128)S(1)} %get-tuple-element.10), channel_id=1, source_target_pairs={{0,3},{1,2},{2,1},{3,0},{4,7},{5,6},{6,5},{7,4},{8,11},{9,10},{10,... | collective-permute-start | bytes 294920 | tf_op jit(solution)/shard_map/ppermute | solution.py:156
  31.5 5.2 %collective-permute-start.4 = (f32[1,16,384]{2,1,0:T(8,128)S(1)}, f32[1,16,384]{2,1,0:T(8,128)S(1)}, u32[]{:S(2)}, u32[]{:S(2)}) collective-permute-start(f32[1,16,384]{2,1,0:T(8,128)S(1)} %get-tuple-element.15), channel_id=1, source_target_pairs={{0,4},{1,5},{2,6},{3,7},{4,0},{5,1},{6,2},{7,3},{8,12},{9,13},{10,... | collective-permute-start | bytes 73736 | tf_op jit(solution)/shard_map/ppermute | solution.py:156
  33.0 5.3 %collective-permute-start.5 = (f32[1,16,384]{2,1,0:T(8,128)S(1)}, f32[1,16,384]{2,1,0:T(8,128)S(1)}, u32[]{:S(2)}, u32[]{:S(2)}) collective-permute-start(f32[1,16,384]{2,1,0:T(8,128)S(1)} %get-tuple-element.14), channel_id=1, source_target_pairs={{0,8},{1,9},{2,10},{3,11},{4,12},{5,13},{6,14},{7,15},{8,0},{9,1},... | collective-permute-start | bytes 73736 | tf_op jit(solution)/shard_map/ppermute | solution.py:156
  35.5 5.6 %collective-permute-start.6 = (f32[1,16,384]{2,1,0:T(8,128)S(1)}, f32[1,16,384]{2,1,0:T(8,128)S(1)}, u32[]{:S(2)}, u32[]{:S(2)}) collective-permute-start(f32[1,16,384]{2,1,0:T(8,128)S(1)} %get-tuple-element.13), channel_id=1, source_target_pairs={{0,12},{1,13},{2,14},{3,15},{4,8},{5,9},{6,10},{7,11},{8,4},{9,5},... | collective-permute-start | bytes 73736 | tf_op jit(solution)/shard_map/ppermute | solution.py:156
